TPU v7x, 32 devices: a whole 2x2x4 slice. The times are simulated.
32 devices in a mesh: groups: 2 (over x), blk: 16 (over z, y, core).
Axes of the slice: x: 2, y: 2, z: 4, core: 2. Of those that a mesh axis runs over, the one named last changes fastest.
Arguments:
- queries: bfloat16 [4096, 4096], P(('groups', 'blk')), parts along dimension 0, may hold values from -96 to 96
- keys: bfloat16 [4096, 512], P(('groups', 'blk')), parts along dimension 0, may hold values from -3 to 3
- values: bfloat16 [4096, 512], P(('groups', 'blk')), parts along dimension 0, may hold values from -4 to 4
- out_packed: int32 [4096, 512], P('blk'), may hold values from -2147483648 to 2147483646
- out_scales: bfloat16 [32, 4096], replicated, may hold values from 0.0029907227 to 0.029907227
- hadamard_signs: int32 [4096], replicated, may hold values from 0 to 1
Outputs:
- mixed: bfloat16 [4096, 4096], P(('groups', 'blk')), parts along dimension 0
There are 2 independent parts, one for each index of `groups`. A program takes and returns all parts, laid end to end along the dimension named above; an argument that names none is the same for every part. Nothing has to cross between parts.
All inputs are finite; a program needn't handle non-finite values.
Results may differ from a plain program's by a relative error of at most 0.012.
Values may be sent and summed in bfloat16 or wider, within the bound.
A program may use at most 256 MiB of HBM per device.

v0:
```python
import math
import jax
import jax.numpy as jnp
from jax import lax
from jax.sharding import PartitionSpec as P

HEAD_SIZE = 128
QUERY_HEADS = 32
KEY_VALUE_HEADS = 4
GROUP = 128
masked_fill_value = -1e30


def sylvester(block_count):
    index = jnp.arange(block_count, dtype=jnp.int32)
    both = jnp.bitwise_and(index[:, None], index[None, :])
    parity = jnp.zeros((block_count, block_count), jnp.int32)
    for bit_number in range(block_count.bit_length() - 1):
        parity = jnp.bitwise_xor(parity, jnp.bitwise_and(jnp.right_shift(both, bit_number), 1))
    return (1 - 2 * parity).astype(jnp.bfloat16)


def rotate(attention, hadamard_signs):
    block_count = attention.shape[0]
    signed = (attention * (2 * hadamard_signs - 1).astype(jnp.bfloat16)).reshape(
        block_count, QUERY_HEADS, HEAD_SIZE
    )
    outer = jnp.einsum(
        "gh,rhd->rgd", sylvester(QUERY_HEADS), signed, preferred_element_type=jnp.float32
    )
    upper = outer.astype(jnp.bfloat16)
    lower = (outer - upper.astype(jnp.float32)).astype(jnp.bfloat16)
    inner_table = sylvester(HEAD_SIZE)
    inner = jnp.einsum("rgd,de->rge", upper, inner_table, preferred_element_type=jnp.float32)
    inner = inner + jnp.einsum(
        "rgd,de->rge", lower, inner_table, preferred_element_type=jnp.float32
    )
    return (
        (inner * (1.0 / math.sqrt(QUERY_HEADS * HEAD_SIZE)))
        .reshape(block_count, QUERY_HEADS * HEAD_SIZE)
        .astype(jnp.bfloat16)
    )


def dequantize_rows(packed, out_scales):
    block_count = packed.shape[0]
    group_count = out_scales.shape[0]
    group_index = jnp.arange(block_count, dtype=jnp.int32) // GROUP
    member = (group_index[:, None] == jnp.arange(group_count, dtype=jnp.int32)[None, :]).astype(
        jnp.bfloat16
    )
    scale_rows = jnp.dot(member, out_scales, preferred_element_type=jnp.float32)
    fields = [jnp.bitwise_and(jnp.right_shift(packed, 4 * nibble), 15) for nibble in range(8)]
    levels = jnp.concatenate(fields, axis=1) - 8
    return (levels.astype(jnp.float32) * scale_rows).astype(jnp.bfloat16)


def update(state, query_tile, query_positions, key_block, value_block, key_positions):
    largest, totals, summed = state
    scores = jnp.einsum("qkgd,nkd->kgqn", query_tile, key_block, preferred_element_type=jnp.float32)
    scores = scores * (1.0 / math.sqrt(HEAD_SIZE))
    allowed = query_positions[:, None] >= key_positions[None, :]
    scores = jnp.where(allowed, scores, masked_fill_value)
    new_largest = jnp.maximum(largest, jnp.max(scores, axis=-1))
    fading = jnp.exp(largest - new_largest)
    weights = jnp.exp(scores - new_largest[..., None])
    totals = totals * fading + jnp.sum(weights, axis=-1)
    product = jnp.einsum(
        "kgqn,nkd->qkgd",
        weights.astype(jnp.bfloat16),
        value_block,
        preferred_element_type=jnp.float32,
    )
    summed = summed * jnp.transpose(fading, (2, 0, 1))[..., None] + product
    return (new_largest, totals, summed)


def keep_state(current):
    return current


def local(queries, keys, values, out_packed, out_scales, hadamard_signs):
    sequence_rows = queries.shape[0]
    my_index = lax.axis_index("blk")
    head_group = QUERY_HEADS // KEY_VALUE_HEADS
    query_positions = my_index * sequence_rows + jnp.arange(sequence_rows, dtype=jnp.int32)
    rows_of_queries = queries.reshape(sequence_rows, KEY_VALUE_HEADS, head_group, HEAD_SIZE)
    initial = (
        jnp.full((KEY_VALUE_HEADS, head_group, sequence_rows), masked_fill_value, jnp.float32),
        jnp.zeros((KEY_VALUE_HEADS, head_group, sequence_rows), jnp.float32),
        jnp.zeros((sequence_rows, KEY_VALUE_HEADS, head_group, HEAD_SIZE), jnp.float32),
    )
    last_position = jnp.max(query_positions)
    key_slice = lax.all_gather(keys, "blk", axis=0, tiled=True)
    value_slice = lax.all_gather(values, "blk", axis=0, tiled=True)
    block_count = key_slice.shape[0]
    width = math.gcd(block_count, 512)
    heads_of_keys = key_slice.reshape(block_count, KEY_VALUE_HEADS, HEAD_SIZE)
    heads_of_values = value_slice.reshape(block_count, KEY_VALUE_HEADS, HEAD_SIZE)

    def sweep(current):

        def one_step(turn, inner_state):
            begin = turn * width
            key_block = lax.dynamic_slice_in_dim(heads_of_keys, begin, width, 0)
            value_block = lax.dynamic_slice_in_dim(heads_of_values, begin, width, 0)
            key_positions = begin + jnp.arange(width, dtype=jnp.int32)
            return update(
                inner_state, rows_of_queries, query_positions, key_block, value_block, key_positions
            )

        return lax.fori_loop(0, block_count // width, one_step, current)

    final = lax.cond(jnp.int32(0) <= last_position, sweep, keep_state, initial)
    largest, totals, summed = final
    attention = (
        (summed / jnp.transpose(totals, (2, 0, 1))[..., None])
        .reshape(sequence_rows, QUERY_HEADS * HEAD_SIZE)
        .astype(jnp.bfloat16)
    )
    rotated = rotate(attention, hadamard_signs)
    weight = dequantize_rows(lax.all_gather(out_packed, "blk", axis=0, tiled=True), out_scales)
    mixed = jnp.dot(rotated, weight, preferred_element_type=jnp.float32)
    return mixed.astype(jnp.bfloat16)


def solution(mesh):
    in_specs = (
        P(("groups", "blk"), None),
        P(("groups", "blk"), None),
        P(("groups", "blk"), None),
        P("blk", None),
        P(),
        P(),
    )
    out_specs = P(("groups", "blk"), None)
    return jax.shard_map(local, mesh=mesh, in_specs=in_specs, out_specs=out_specs, check_vma=False)
```

profile of v0, /device:TPU:0, one launch (start us, length us, event | category | flops | bytes accessed | tf_op | source)
XLA Modules:
  0.0 240.5 jit_solution(12664698832807533376)
XLA Ops:
  6.5 1.7 copy.25
  8.3 1.7 copy.26
  12.6 40.6 %all-gather.4.cloned.1.call-done = bf16[2048,512]{0,1:T(8,128)(2,1)} async-done(((bf16[128,512]{0,1:T(8,128)(2,1)}), bf16[2048,512]{0,1:T(8,128)(2,1)}) %all-gather.4.cloned.1.call-update) | async-done | bytes 2097168 | tf_op jit(solution)/shard_map/all_gather | solution.py:94
  53.3 42.3 %all-gather.6.cloned.1.call-done = bf16[2048,512]{0,1:T(8,128)(2,1)} async-done(((bf16[128,512]{0,1:T(8,128)(2,1)}), bf16[2048,512]{0,1:T(8,128)(2,1)}) %all-gather.6.cloned.1.call-update) | async-done | bytes 2097168 | tf_op jit(solution)/shard_map/all_gather | solution.py:95
  95.6 69.5 %conditional.1 = (f32[4,8,128]{2,1,0:T(8,128)}, f32[128,4,8,128]{0,3,2,1:T(8,128)}) conditional(s32[]{:T(128)} %convert_element_type.53, () %tuple.27, (bf16[2048,512]{0,1:T(8,128)(2,1)}, bf16[2048,512]{0,1:T(8,128)(2,1)}, bf16[128,4096]{1,0:T(8,128)(2,1)}, s32[128]{0:T(128)S(1)}) %tuple.28), branch_computations={%region_1.0_spmd, %region_2.7_spmd} | conditional | flops 1098473984 | bytes 69735248 | solution.py:114
  95.6 1.6 copy.27
  97.9 67.2 %while.17 = (s32[]{:T(128)}, f32[4,8,128]{2,1,0:T(8,128)S(1)}, f32[4,8,128]{2,1,0:T(8,128)}, f32[128,4,8,128]{0,3,2,1:T(8,128)}, s32[128]{0:T(128)S(1)}, /*index...) while((s32[]{:T(128)}, f32[4,8,128]{2,1,0:T(8,128)S(1)}, ...), condition=%wide.region_6.6_spmd.clone, body=%wide.region_3.5_spmd.clone.sunk | while | flops 1098473984 | bytes 65540820 | solution.py:112
  98.1 5.7 %fusion.87 = (f32[4,8,128]{2,1,0:T(8,128)S(1)}, f32[4,512,128,8]{2,1,3,0:T(8,128)}) fusion(pred[128,512]{0,1:T(8,128)(4,1)S(1)} %broadcast_compare_fusion.2, bf16[128,4,8,128]{3,0,2,1:T(8,128)(2,1)S(1)} %get-tuple-element.326, bf16[2048,4,128]{0,2,1:T(8,128)(2,1)} %get-tuple-element.325, s32[]{:T(128)S(6)} %select_n.46), kind=kOutput, calls=%fused_computation.4.clone.1 | convolution fusion | flops 543158272 | bytes 10043396 | tf_op jit(solution)/shard_map/cond/branch_1_fun/while/body/eval_jaxpr/qkgd,nkd->kgqn/dot_general | solution.py:60
  103.8 7.6 %bitcast_add_fusion.2 = f32[128,4,8,128]{0,3,2,1:T(8,128)} fusion(f32[128,4,8,128]{0,3,2,1:T(8,128)} %get-tuple-element.311, f32[4,512,128,8]{2,1,3,0:T(8,128)} %get-tuple-element.294, f32[4,8,128]{2,1,0:T(8,128)S(1)} %get-tuple-element.321, pred[128,512]{0,1:T(8,128)(4,1)S(1)} %broadcast_compare_fusion.2, f32[128,4,8]{0,2,1:T(8,128)S(1)} %get-tuple-element.295, ...), kind=kOutput, calls=%fused_computation.10.clone.1 | convolution fusion | flops 546832384 | bytes 13205509 | tf_op jit(solution)/shard_map/cond/branch_1_fun/while/body/eval_jaxpr/kgqn,nkd->qkgd/dot_general | solution.py:68
  111.4 1.8 fusion.89
  114.0 5.7 %fusion.87 = (f32[4,8,128]{2,1,0:T(8,128)S(1)}, f32[4,512,128,8]{2,1,3,0:T(8,128)}) fusion(pred[128,512]{0,1:T(8,128)(4,1)S(1)} %broadcast_compare_fusion.2, bf16[128,4,8,128]{3,0,2,1:T(8,128)(2,1)S(1)} %get-tuple-element.326, bf16[2048,4,128]{0,2,1:T(8,128)(2,1)} %get-tuple-element.325, s32[]{:T(128)S(6)} %select_n.46), kind=kOutput, calls=%fused_computation.4.clone.1 | convolution fusion | flops 543158272 | bytes 10043396 | tf_op jit(solution)/shard_map/cond/branch_1_fun/while/body/eval_jaxpr/qkgd,nkd->kgqn/dot_general | solution.py:60
  119.8 7.9 %bitcast_add_fusion.2 = f32[128,4,8,128]{0,3,2,1:T(8,128)} fusion(f32[128,4,8,128]{0,3,2,1:T(8,128)} %get-tuple-element.311, f32[4,512,128,8]{2,1,3,0:T(8,128)} %get-tuple-element.294, f32[4,8,128]{2,1,0:T(8,128)S(1)} %get-tuple-element.321, pred[128,512]{0,1:T(8,128)(4,1)S(1)} %broadcast_compare_fusion.2, f32[128,4,8]{0,2,1:T(8,128)S(1)} %get-tuple-element.295, ...), kind=kOutput, calls=%fused_computation.10.clone.1 | convolution fusion | flops 546832384 | bytes 13205509 | tf_op jit(solution)/shard_map/cond/branch_1_fun/while/body/eval_jaxpr/kgqn,nkd->qkgd/dot_general | solution.py:68
  127.6 1.8 fusion.89
  129.4 1.3 fusion.90
  130.9 5.8 %fusion.87 = (f32[4,8,128]{2,1,0:T(8,128)S(1)}, f32[4,512,128,8]{2,1,3,0:T(8,128)}) fusion(pred[128,512]{0,1:T(8,128)(4,1)S(1)} %broadcast_compare_fusion.2, bf16[128,4,8,128]{3,0,2,1:T(8,128)(2,1)S(1)} %get-tuple-element.326, bf16[2048,4,128]{0,2,1:T(8,128)(2,1)} %get-tuple-element.325, s32[]{:T(128)S(6)} %select_n.46), kind=kOutput, calls=%fused_computation.4.clone.1 | convolution fusion | flops 543158272 | bytes 10043396 | tf_op jit(solution)/shard_map/cond/branch_1_fun/while/body/eval_jaxpr/qkgd,nkd->kgqn/dot_general | solution.py:60
  136.7 8.0 %bitcast_add_fusion.2 = f32[128,4,8,128]{0,3,2,1:T(8,128)} fusion(f32[128,4,8,128]{0,3,2,1:T(8,128)} %get-tuple-element.311, f32[4,512,128,8]{2,1,3,0:T(8,128)} %get-tuple-element.294, f32[4,8,128]{2,1,0:T(8,128)S(1)} %get-tuple-element.321, pred[128,512]{0,1:T(8,128)(4,1)S(1)} %broadcast_compare_fusion.2, f32[128,4,8]{0,2,1:T(8,128)S(1)} %get-tuple-element.295, ...), kind=kOutput, calls=%fused_computation.10.clone.1 | convolution fusion | flops 546832384 | bytes 13205509 | tf_op jit(solution)/shard_map/cond/branch_1_fun/while/body/eval_jaxpr/kgqn,nkd->qkgd/dot_general | solution.py:68
  144.7 1.8 fusion.89
  146.5 1.3 fusion.90
  148.0 5.7 %fusion.87 = (f32[4,8,128]{2,1,0:T(8,128)S(1)}, f32[4,512,128,8]{2,1,3,0:T(8,128)}) fusion(pred[128,512]{0,1:T(8,128)(4,1)S(1)} %broadcast_compare_fusion.2, bf16[128,4,8,128]{3,0,2,1:T(8,128)(2,1)S(1)} %get-tuple-element.326, bf16[2048,4,128]{0,2,1:T(8,128)(2,1)} %get-tuple-element.325, s32[]{:T(128)S(6)} %select_n.46), kind=kOutput, calls=%fused_computation.4.clone.1 | convolution fusion | flops 543158272 | bytes 10043396 | tf_op jit(solution)/shard_map/cond/branch_1_fun/while/body/eval_jaxpr/qkgd,nkd->kgqn/dot_general | solution.py:60
  153.7 8.2 %bitcast_add_fusion.2 = f32[128,4,8,128]{0,3,2,1:T(8,128)} fusion(f32[128,4,8,128]{0,3,2,1:T(8,128)} %get-tuple-element.311, f32[4,512,128,8]{2,1,3,0:T(8,128)} %get-tuple-element.294, f32[4,8,128]{2,1,0:T(8,128)S(1)} %get-tuple-element.321, pred[128,512]{0,1:T(8,128)(4,1)S(1)} %broadcast_compare_fusion.2, f32[128,4,8]{0,2,1:T(8,128)S(1)} %get-tuple-element.295, ...), kind=kOutput, calls=%fused_computation.10.clone.1 | convolution fusion | flops 546832384 | bytes 13205509 | tf_op jit(solution)/shard_map/cond/branch_1_fun/while/body/eval_jaxpr/kgqn,nkd->qkgd/dot_general | solution.py:68
  161.9 1.8 fusion.89
  165.1 1.8 divide_convert_fusion
  169.6 1.6 all-gather.8.cloned.1.call-done
  171.2 7.8 %and_dynamic-update-slice_fusion.7 = s32[4096,4096]{1,0:T(8,128)} fusion(s32[4096,512]{1,0:T(8,128)} %all-gather.8.cloned.1.call-done), kind=kLoop, calls=%fused_computation.37 | loop fusion | flops 4194303 | bytes 16777216
  179.0 4.3 %and_dynamic-update-slice_fusion.6 = s32[4096,4096]{1,0:T(8,128)} fusion(s32[4096,4096]{1,0:T(8,128)} %and_dynamic-update-slice_fusion.7, s32[4096,512]{1,0:T(8,128)S(1)} %copy-done.2), kind=kLoop, calls=%fused_computation.36 | loop fusion | flops 4194304 | bytes 16777216
  183.3 4.3 %and_dynamic-update-slice_fusion.5 = s32[4096,4096]{1,0:T(8,128)} fusion(s32[4096,4096]{1,0:T(8,128)} %and_dynamic-update-slice_fusion.6, s32[4096,512]{1,0:T(8,128)S(1)} %copy-done.2), kind=kLoop, calls=%fused_computation.35 | loop fusion | flops 4194304 | bytes 16777216
  187.5 4.2 %and_dynamic-update-slice_fusion.4 = s32[4096,4096]{1,0:T(8,128)} fusion(s32[4096,4096]{1,0:T(8,128)} %and_dynamic-update-slice_fusion.5, s32[4096,512]{1,0:T(8,128)S(1)} %copy-done.2), kind=kLoop, calls=%fused_computation.34 | loop fusion | flops 4194304 | bytes 16777216
  191.8 4.3 %and_dynamic-update-slice_fusion.3 = s32[4096,4096]{1,0:T(8,128)} fusion(s32[4096,4096]{1,0:T(8,128)} %and_dynamic-update-slice_fusion.4, s32[4096,512]{1,0:T(8,128)S(1)} %copy-done.2), kind=kLoop, calls=%fused_computation.33 | loop fusion | flops 4194304 | bytes 16777216
  196.0 4.2 %and_dynamic-update-slice_fusion.2 = s32[4096,4096]{1,0:T(8,128)} fusion(s32[4096,4096]{1,0:T(8,128)} %and_dynamic-update-slice_fusion.3, s32[4096,512]{1,0:T(8,128)S(1)} %copy-done.2), kind=kLoop, calls=%fused_computation.32 | loop fusion | flops 4194304 | bytes 16777216
  200.3 4.3 %and_dynamic-update-slice_fusion.1 = s32[4096,4096]{1,0:T(8,128)} fusion(s32[4096,4096]{1,0:T(8,128)} %and_dynamic-update-slice_fusion.2, s32[4096,512]{1,0:T(8,128)S(1)} %copy-done.2), kind=kLoop, calls=%fused_computation.31 | loop fusion | flops 4194304 | bytes 16777216
  204.6 4.3 %and_dynamic-update-slice_fusion = s32[4096,4096]{1,0:T(8,128)} fusion(s32[4096,4096]{1,0:T(8,128)} %and_dynamic-update-slice_fusion.1, s32[4096,512]{1,0:T(8,128)S(1)} %copy-done.2), kind=kLoop, calls=%fused_computation.30 | loop fusion | flops 4194304 | bytes 16777216 | tf_op jit(solution)/shard_map/concatenate | solution.py:54
  208.9 25.0 %fusion.23 = bf16[128,4096]{1,0:T(8,128)(2,1)} fusion(bf16[128,4096]{0,1:T(8,128)(2,1)S(1)} %bitcast.70, s32[4096,4096]{1,0:T(8,128)} %and_dynamic-update-slice_fusion, bf16[32,4096]{1,0:T(8,128)(2,1)S(1)} %copy-done, s32[4096]{0:T(1024)S(1)} %add_select_fusion), kind=kOutput, calls=%fused_computation.38 | convolution fusion | flops 5436473344 | bytes 69484544 | tf_op jit(solution)/shard_map/dot_general | solution.py:123
  (48 shorter events, 8.1 us)
Async XLA Ops:
  6.5 202.4 %copy-start = (bf16[32,4096]{1,0:T(8,128)(2,1)S(1)}, bf16[32,4096]{1,0:T(8,128)(2,1)}, u32[]{:S(2)}) copy-start(bf16[32,4096]{1,0:T(8,128)(2,1)} %param.14) | copy-start | bytes 786436
  6.5 46.7 %all-gather.4.cloned.1.call-start = ((), (), s32[]{:S(2)}) async-start(), calls=%async_computation | async-start | bytes 2228224 | tf_op jit(solution)/shard_map/all_gather | solution.py:94
  8.3 87.3 %all-gather.6.cloned.1.call-start = ((), (), s32[]{:S(2)}) async-start(), calls=%async_computation.1 | async-start | bytes 2228224 | tf_op jit(solution)/shard_map/all_gather | solution.py:95
  10.0 161.2 %all-gather.8.cloned.1.call-start = ((), (), s32[]{:S(2)}) async-start(), calls=%async_computation.2 | async-start | bytes 8912896 | tf_op jit(solution)/shard_map/all_gather | solution.py:122
  103.8 7.6 %copy-start.1 = (f32[4,512,128,8]{2,1,3,0:T(8,128)S(1)}, f32[4,512,128,8]{2,1,3,0:T(8,128)}, u32[]{:S(2)}) copy-start(f32[4,512,128,8]{2,1,3,0:T(8,128)} %get-tuple-element.294) | copy-start | bytes 25165828 | tf_op jit(solution)/shard_map/cond/branch_1_fun/while
  119.7 7.9 %copy-start.1 = (f32[4,512,128,8]{2,1,3,0:T(8,128)S(1)}, f32[4,512,128,8]{2,1,3,0:T(8,128)}, u32[]{:S(2)}) copy-start(f32[4,512,128,8]{2,1,3,0:T(8,128)} %get-tuple-element.294) | copy-start | bytes 25165828 | tf_op jit(solution)/shard_map/cond/branch_1_fun/while
  136.7 8.0 %copy-start.1 = (f32[4,512,128,8]{2,1,3,0:T(8,128)S(1)}, f32[4,512,128,8]{2,1,3,0:T(8,128)}, u32[]{:S(2)}) copy-start(f32[4,512,128,8]{2,1,3,0:T(8,128)} %get-tuple-element.294) | copy-start | bytes 25165828 | tf_op jit(solution)/shard_map/cond/branch_1_fun/while
  153.7 8.2 %copy-start.1 = (f32[4,512,128,8]{2,1,3,0:T(8,128)S(1)}, f32[4,512,128,8]{2,1,3,0:T(8,128)}, u32[]{:S(2)}) copy-start(f32[4,512,128,8]{2,1,3,0:T(8,128)} %get-tuple-element.294) | copy-start | bytes 25165828 | tf_op jit(solution)/shard_map/cond/branch_1_fun/while
  171.2 7.8 %copy-start.2 = (s32[4096,512]{1,0:T(8,128)S(1)}, s32[4096,512]{1,0:T(8,128)}, u32[]{:S(2)}) copy-start(s32[4096,512]{1,0:T(8,128)} %all-gather.8.cloned.1.call-done) | copy-start | bytes 25165828
Sparse Core Ops, SparseCore 0:
  9.5 43.7 all-gather.3
  55.4 40.1 all-gather.5
  97.8 73.3 all-gather.7
where the time goes:
time: 241 us; the launch traced here: 240 us
  waiting for transfers between devices  85.2 us (35%)
  matrix products  81.3 us (34%)
  other arithmetic  53.4 us (22%)
  between operations  13.7 us (6%)
  local copies, waits for them, and re-layouts  6.64 us (3%)
    all_gather x1, waiting for transfers between devices, local(): value_slice = lax.all_gather(values, 'blk', axis=0, tiled=True)  42.3 us
    all_gather x1, waiting for transfers between devices, local(): key_slice = lax.all_gather(keys, 'blk', axis=0, tiled=True)  40.6 us
    unnamed x7, other arithmetic  33.4 us
    dot_general x4, matrix products, update(): jnp.einsum('kgqn,nkd->qkgd', weights.astype(jnp.bfloat16), value_block, p...  31.6 us
    dot_general x1, matrix products, local(): mixed = jnp.dot(rotated, weight, preferred_element_type=jnp.float32)  25 us
    dot_general x4, matrix products, update(): jnp.einsum('qkgd,nkd->kgqn', query_tile, key_block, preferred_element_typ...  22.9 us
    reduce_sum x4, other arithmetic, update(): totals = totals * fading + jnp.sum(weights, axis=-1)  7.23 us
  transfers between devices with their start and end apart: 3, of which 3 were waited for; matrix products, arithmetic and copies ran while one was open for 32% of the time, Pallas kernels for 0%

commit v1 on v0

--- a/solution.py
+++ b/solution.py
@@ -91,8 +91,11 @@
         jnp.zeros((sequence_rows, KEY_VALUE_HEADS, head_group, HEAD_SIZE), jnp.float32),
     )
     last_position = jnp.max(query_positions)
-    key_slice = lax.all_gather(keys, "blk", axis=0, tiled=True)
-    value_slice = lax.all_gather(values, "blk", axis=0, tiled=True)
+    key_slice, value_slice = jnp.split(
+        lax.all_gather(jnp.concatenate([keys, values], axis=1), "blk", axis=0, tiled=True),
+        [keys.shape[1]],
+        axis=1,
+    )
     block_count = key_slice.shape[0]
     width = math.gcd(block_count, 512)
     heads_of_keys = key_slice.reshape(block_count, KEY_VALUE_HEADS, HEAD_SIZE)

time: 241 us -> 210 us (0.87)
  waiting for transfers between devices: 85.2 us -> 53.7 us
  matrix products: 81.3 us -> 76.6 us
  local copies, waits for them, and re-layouts: 6.64 us -> 10.1 us
    all_gather x2 -> x1, waiting for transfers between devices: 82.9 us -> 52.5 us  [local(): lax.all_gather(jnp.concatenate([keys, values], axis=1), 'blk', axis=0, ti...]
    dot_general x4, matrix products: 22.9 us -> 18.7 us  [update(): jnp.einsum('qkgd,nkd->kgqn', query_tile, key_block, preferred_element_typ...]
    split x0 -> x1, local copies, waits for them, and re-layouts: none -> 4.08 us  [local(): jnp.split(lax.all_gather(jnp.concatenate([keys, values], axis=1), 'blk',...]
  transfers between devices with their start and end apart: 3 -> 2, of which waited for: 3 -> 2; matrix products, arithmetic and copies ran while one was open for 32% -> 36% of each run, Pallas kernels for 0% -> 0%
where the time goes in v1:
time: 210 us; the launch traced here: 209 us
  matrix products  76.6 us (36%)
  other arithmetic  54.3 us (26%)
  waiting for transfers between devices  53.7 us (26%)
  between operations  14.2 us (7%)
  local copies, waits for them, and re-layouts  10.1 us (5%)
    all_gather x1, waiting for transfers between devices, local(): lax.all_gather(jnp.concatenate([keys, values], axis=1), 'blk', axis=0, ti...  52.5 us
    unnamed x7, other arithmetic  33.4 us
    dot_general x4, matrix products, update(): jnp.einsum('kgqn,nkd->qkgd', weights.astype(jnp.bfloat16), value_block, p...  31.1 us
    dot_general x1, matrix products, local(): mixed = jnp.dot(rotated, weight, preferred_element_type=jnp.float32)  25 us
    dot_general x4, matrix products, update(): jnp.einsum('qkgd,nkd->kgqn', query_tile, key_block, preferred_element_typ...  18.7 us
    reduce_sum x4, other arithmetic, update(): totals = totals * fading + jnp.sum(weights, axis=-1)  7.23 us
    add x4, other arithmetic, update(): totals = totals * fading + jnp.sum(weights, axis=-1)  4.67 us
    concatenate x1, other arithmetic, dequantize_rows(): levels = jnp.concatenate(fields, axis=1) - 8  4.28 us
  transfers between devices with their start and end apart: 2, of which 2 were waited for; matrix products, arithmetic and copies ran while one was open for 36% of the time, Pallas kernels for 0%

profile of v1, /device:TPU:0, one launch (start us, length us, event | category | flops | bytes accessed | tf_op | source)
XLA Modules:
  0.0 209.0 jit_solution(16537927073208589743)
XLA Ops:
  6.5 1.1 copy.26
  12.3 52.5 %all-gather.3.cloned.1.call-done = bf16[2048,1024]{0,1:T(8,128)(2,1)} async-done(((bf16[128,1024]{0,1:T(8,128)(2,1)}), bf16[2048,1024]{0,1:T(8,128)(2,1)}) %all-gather.3.cloned.1.call-update) | async-done | bytes 4194320 | tf_op jit(solution)/shard_map/all_gather | solution.py:95
  64.8 69.5 %conditional.1 = (f32[4,8,128]{2,1,0:T(8,128)}, f32[128,4,8,128]{0,3,2,1:T(8,128)}) conditional(s32[]{:T(128)} %convert_element_type.53, () %tuple.27, (bf16[2048,1024]{0,1:T(8,128)(2,1)}, bf16[128,4096]{1,0:T(8,128)(2,1)}, s32[128]{0:T(128)S(1)}) %tuple.28), branch_computations={%region_1.0_spmd, %region_2.7_spmd} | conditional | flops 1098473984 | bytes 82318184 | solution.py:117
  64.8 4.1 %fusion.74 = (bf16[2048,512]{0,1:T(8,128)(2,1)}, bf16[2048,512]{0,1:T(8,128)(2,1)S(1)}) fusion(bf16[2048,1024]{0,1:T(8,128)(2,1)} %get-tuple-element.156), kind=kLoop, calls=%fused_computation.99 | loop fusion | bytes 8388608 | tf_op jit(solution)/shard_map/split | solution.py:94
  68.8 1.3 copy.28
  70.1 1.6 copy.25
  71.8 62.5 %while.17 = (s32[]{:T(128)}, f32[4,8,128]{2,1,0:T(8,128)S(1)}, f32[4,8,128]{2,1,0:T(8,128)}, f32[128,4,8,128]{0,3,2,1:T(8,128)}, s32[128]{0:T(128)S(1)}, /*index...) while((s32[]{:T(128)}, f32[4,8,128]{2,1,0:T(8,128)S(1)}, ...), condition=%wide.region_6.6_spmd.clone, body=%wide.region_3.5_spmd.clone.sunk | while | flops 1098473984 | bytes 65540820 | solution.py:115
  72.0 4.7 %fusion.88 = (f32[4,8,128]{2,1,0:T(8,128)S(1)}, f32[4,512,128,8]{2,1,3,0:T(8,128)}) fusion(pred[128,512]{0,1:T(8,128)(4,1)S(1)} %broadcast_compare_fusion.2, bf16[128,4,8,128]{3,0,2,1:T(8,128)(2,1)S(1)} %get-tuple-element.326, bf16[2048,4,128]{0,2,1:T(8,128)(2,1)S(1)} %get-tuple-element.325, s32[]{:T(128)S(6)} %select_n.46), kind=kOutput, calls=%fused_computation.4.clone.1 | convolution fusion | flops 543158272 | bytes 10043396 | tf_op jit(solution)/shard_map/cond/branch_1_fun/while/body/eval_jaxpr/qkgd,nkd->kgqn/dot_general | solution.py:60
  76.7 7.2 %bitcast_add_fusion.2 = f32[128,4,8,128]{0,3,2,1:T(8,128)} fusion(f32[128,4,8,128]{0,3,2,1:T(8,128)} %get-tuple-element.311, f32[4,512,128,8]{2,1,3,0:T(8,128)} %get-tuple-element.294, f32[4,8,128]{2,1,0:T(8,128)S(1)} %get-tuple-element.321, pred[128,512]{0,1:T(8,128)(4,1)S(1)} %broadcast_compare_fusion.2, f32[128,4,8]{0,2,1:T(8,128)S(1)} %get-tuple-element.295, ...), kind=kOutput, calls=%fused_computation.10.clone.1 | convolution fusion | flops 546832384 | bytes 13205509 | tf_op jit(solution)/shard_map/cond/branch_1_fun/while/body/eval_jaxpr/kgqn,nkd->qkgd/dot_general | solution.py:68
  83.9 1.8 fusion.90
  86.5 4.7 %fusion.88 = (f32[4,8,128]{2,1,0:T(8,128)S(1)}, f32[4,512,128,8]{2,1,3,0:T(8,128)}) fusion(pred[128,512]{0,1:T(8,128)(4,1)S(1)} %broadcast_compare_fusion.2, bf16[128,4,8,128]{3,0,2,1:T(8,128)(2,1)S(1)} %get-tuple-element.326, bf16[2048,4,128]{0,2,1:T(8,128)(2,1)S(1)} %get-tuple-element.325, s32[]{:T(128)S(6)} %select_n.46), kind=kOutput, calls=%fused_computation.4.clone.1 | convolution fusion | flops 543158272 | bytes 10043396 | tf_op jit(solution)/shard_map/cond/branch_1_fun/while/body/eval_jaxpr/qkgd,nkd->kgqn/dot_general | solution.py:60
  91.2 7.8 %bitcast_add_fusion.2 = f32[128,4,8,128]{0,3,2,1:T(8,128)} fusion(f32[128,4,8,128]{0,3,2,1:T(8,128)} %get-tuple-element.311, f32[4,512,128,8]{2,1,3,0:T(8,128)} %get-tuple-element.294, f32[4,8,128]{2,1,0:T(8,128)S(1)} %get-tuple-element.321, pred[128,512]{0,1:T(8,128)(4,1)S(1)} %broadcast_compare_fusion.2, f32[128,4,8]{0,2,1:T(8,128)S(1)} %get-tuple-element.295, ...), kind=kOutput, calls=%fused_computation.10.clone.1 | convolution fusion | flops 546832384 | bytes 13205509 | tf_op jit(solution)/shard_map/cond/branch_1_fun/while/body/eval_jaxpr/kgqn,nkd->qkgd/dot_general | solution.py:68
  99.0 1.8 fusion.90
  100.8 1.3 fusion.91
  102.3 4.7 %fusion.88 = (f32[4,8,128]{2,1,0:T(8,128)S(1)}, f32[4,512,128,8]{2,1,3,0:T(8,128)}) fusion(pred[128,512]{0,1:T(8,128)(4,1)S(1)} %broadcast_compare_fusion.2, bf16[128,4,8,128]{3,0,2,1:T(8,128)(2,1)S(1)} %get-tuple-element.326, bf16[2048,4,128]{0,2,1:T(8,128)(2,1)S(1)} %get-tuple-element.325, s32[]{:T(128)S(6)} %select_n.46), kind=kOutput, calls=%fused_computation.4.clone.1 | convolution fusion | flops 543158272 | bytes 10043396 | tf_op jit(solution)/shard_map/cond/branch_1_fun/while/body/eval_jaxpr/qkgd,nkd->kgqn/dot_general | solution.py:60
  107.0 7.9 %bitcast_add_fusion.2 = f32[128,4,8,128]{0,3,2,1:T(8,128)} fusion(f32[128,4,8,128]{0,3,2,1:T(8,128)} %get-tuple-element.311, f32[4,512,128,8]{2,1,3,0:T(8,128)} %get-tuple-element.294, f32[4,8,128]{2,1,0:T(8,128)S(1)} %get-tuple-element.321, pred[128,512]{0,1:T(8,128)(4,1)S(1)} %broadcast_compare_fusion.2, f32[128,4,8]{0,2,1:T(8,128)S(1)} %get-tuple-element.295, ...), kind=kOutput, calls=%fused_computation.10.clone.1 | convolution fusion | flops 546832384 | bytes 13205509 | tf_op jit(solution)/shard_map/cond/branch_1_fun/while/body/eval_jaxpr/kgqn,nkd->qkgd/dot_general | solution.py:68
  114.9 1.8 fusion.90
  116.7 1.3 fusion.91
  118.2 4.7 %fusion.88 = (f32[4,8,128]{2,1,0:T(8,128)S(1)}, f32[4,512,128,8]{2,1,3,0:T(8,128)}) fusion(pred[128,512]{0,1:T(8,128)(4,1)S(1)} %broadcast_compare_fusion.2, bf16[128,4,8,128]{3,0,2,1:T(8,128)(2,1)S(1)} %get-tuple-element.326, bf16[2048,4,128]{0,2,1:T(8,128)(2,1)S(1)} %get-tuple-element.325, s32[]{:T(128)S(6)} %select_n.46), kind=kOutput, calls=%fused_computation.4.clone.1 | convolution fusion | flops 543158272 | bytes 10043396 | tf_op jit(solution)/shard_map/cond/branch_1_fun/while/body/eval_jaxpr/qkgd,nkd->kgqn/dot_general | solution.py:60
  122.9 8.2 %bitcast_add_fusion.2 = f32[128,4,8,128]{0,3,2,1:T(8,128)} fusion(f32[128,4,8,128]{0,3,2,1:T(8,128)} %get-tuple-element.311, f32[4,512,128,8]{2,1,3,0:T(8,128)} %get-tuple-element.294, f32[4,8,128]{2,1,0:T(8,128)S(1)} %get-tuple-element.321, pred[128,512]{0,1:T(8,128)(4,1)S(1)} %broadcast_compare_fusion.2, f32[128,4,8]{0,2,1:T(8,128)S(1)} %get-tuple-element.295, ...), kind=kOutput, calls=%fused_computation.10.clone.1 | convolution fusion | flops 546832384 | bytes 13205509 | tf_op jit(solution)/shard_map/cond/branch_1_fun/while/body/eval_jaxpr/kgqn,nkd->qkgd/dot_general | solution.py:68
  131.1 1.8 fusion.90
  132.9 1.3 fusion.91
  134.3 2.0 divide_convert_fusion
  139.4 7.9 %and_dynamic-update-slice_fusion.7 = s32[4096,4096]{1,0:T(8,128)} fusion(s32[4096,512]{1,0:T(8,128)} %all-gather.5.cloned.1.call-done), kind=kLoop, calls=%fused_computation.37 | loop fusion | flops 4194303 | bytes 16777216
  147.3 4.3 %and_dynamic-update-slice_fusion.6 = s32[4096,4096]{1,0:T(8,128)} fusion(s32[4096,4096]{1,0:T(8,128)} %and_dynamic-update-slice_fusion.7, s32[4096,512]{1,0:T(8,128)S(1)} %copy-done.2), kind=kLoop, calls=%fused_computation.36 | loop fusion | flops 4194304 | bytes 16777216
  151.6 4.3 %and_dynamic-update-slice_fusion.5 = s32[4096,4096]{1,0:T(8,128)} fusion(s32[4096,4096]{1,0:T(8,128)} %and_dynamic-update-slice_fusion.6, s32[4096,512]{1,0:T(8,128)S(1)} %copy-done.2), kind=kLoop, calls=%fused_computation.35 | loop fusion | flops 4194304 | bytes 16777216
  155.8 4.3 %and_dynamic-update-slice_fusion.4 = s32[4096,4096]{1,0:T(8,128)} fusion(s32[4096,4096]{1,0:T(8,128)} %and_dynamic-update-slice_fusion.5, s32[4096,512]{1,0:T(8,128)S(1)} %copy-done.2), kind=kLoop, calls=%fused_computation.34 | loop fusion | flops 4194304 | bytes 16777216
  160.1 4.2 %and_dynamic-update-slice_fusion.3 = s32[4096,4096]{1,0:T(8,128)} fusion(s32[4096,4096]{1,0:T(8,128)} %and_dynamic-update-slice_fusion.4, s32[4096,512]{1,0:T(8,128)S(1)} %copy-done.2), kind=kLoop, calls=%fused_computation.33 | loop fusion | flops 4194304 | bytes 16777216
  164.3 4.3 %and_dynamic-update-slice_fusion.2 = s32[4096,4096]{1,0:T(8,128)} fusion(s32[4096,4096]{1,0:T(8,128)} %and_dynamic-update-slice_fusion.3, s32[4096,512]{1,0:T(8,128)S(1)} %copy-done.2), kind=kLoop, calls=%fused_computation.32 | loop fusion | flops 4194304 | bytes 16777216
  168.6 4.2 %and_dynamic-update-slice_fusion.1 = s32[4096,4096]{1,0:T(8,128)} fusion(s32[4096,4096]{1,0:T(8,128)} %and_dynamic-update-slice_fusion.2, s32[4096,512]{1,0:T(8,128)S(1)} %copy-done.2), kind=kLoop, calls=%fused_computation.31 | loop fusion | flops 4194304 | bytes 16777216
  172.8 4.3 %and_dynamic-update-slice_fusion = s32[4096,4096]{1,0:T(8,128)} fusion(s32[4096,4096]{1,0:T(8,128)} %and_dynamic-update-slice_fusion.1, s32[4096,512]{1,0:T(8,128)S(1)} %copy-done.2), kind=kLoop, calls=%fused_computation.30 | loop fusion | flops 4194304 | bytes 16777216 | tf_op jit(solution)/shard_map/concatenate | solution.py:54
  177.1 25.0 %fusion.23 = bf16[128,4096]{1,0:T(8,128)(2,1)} fusion(bf16[128,4096]{0,1:T(8,128)(2,1)S(1)} %bitcast.71, s32[4096,4096]{1,0:T(8,128)} %and_dynamic-update-slice_fusion, bf16[32,4096]{1,0:T(8,128)(2,1)S(1)} %copy-done, s32[4096]{0:T(1024)S(1)} %add_select_fusion), kind=kOutput, calls=%fused_computation.38 | convolution fusion | flops 5436473344 | bytes 69484544 | tf_op jit(solution)/shard_map/dot_general | solution.py:126
  (49 shorter events, 8.4 us)
Async XLA Ops:
  6.5 170.6 %copy-start = (bf16[32,4096]{1,0:T(8,128)(2,1)S(1)}, bf16[32,4096]{1,0:T(8,128)(2,1)}, u32[]{:S(2)}) copy-start(bf16[32,4096]{1,0:T(8,128)(2,1)} %param.14) | copy-start | bytes 786436
  6.5 58.2 %all-gather.3.cloned.1.call-start = ((), (), s32[]{:S(2)}) async-start(), calls=%async_computation | async-start | bytes 4456448 | tf_op jit(solution)/shard_map/all_gather | solution.py:95
  9.4 130.0 %all-gather.5.cloned.1.call-start = ((), (), s32[]{:S(2)}) async-start(), calls=%async_computation.1 | async-start | bytes 8912896 | tf_op jit(solution)/shard_map/all_gather | solution.py:125
  64.8 4.1 %copy-start.3 = (bf16[128,4096]{1,0:T(8,128)(2,1)S(1)}, bf16[128,4096]{1,0:T(8,128)(2,1)}, u32[]{:S(2)}) copy-start(bf16[128,4096]{1,0:T(8,128)(2,1)} %get-tuple-element.213) | copy-start | bytes 3145732 | tf_op jit(solution)/shard_map/cond
  76.6 7.3 %copy-start.1 = (f32[4,512,128,8]{2,1,3,0:T(8,128)S(1)}, f32[4,512,128,8]{2,1,3,0:T(8,128)}, u32[]{:S(2)}) copy-start(f32[4,512,128,8]{2,1,3,0:T(8,128)} %get-tuple-element.294) | copy-start | bytes 25165828 | tf_op jit(solution)/shard_map/cond/branch_1_fun/while
  91.2 7.8 %copy-start.1 = (f32[4,512,128,8]{2,1,3,0:T(8,128)S(1)}, f32[4,512,128,8]{2,1,3,0:T(8,128)}, u32[]{:S(2)}) copy-start(f32[4,512,128,8]{2,1,3,0:T(8,128)} %get-tuple-element.294) | copy-start | bytes 25165828 | tf_op jit(solution)/shard_map/cond/branch_1_fun/while
  107.0 7.9 %copy-start.1 = (f32[4,512,128,8]{2,1,3,0:T(8,128)S(1)}, f32[4,512,128,8]{2,1,3,0:T(8,128)}, u32[]{:S(2)}) copy-start(f32[4,512,128,8]{2,1,3,0:T(8,128)} %get-tuple-element.294) | copy-start | bytes 25165828 | tf_op jit(solution)/shard_map/cond/branch_1_fun/while
  122.9 8.2 %copy-start.1 = (f32[4,512,128,8]{2,1,3,0:T(8,128)S(1)}, f32[4,512,128,8]{2,1,3,0:T(8,128)}, u32[]{:S(2)}) copy-start(f32[4,512,128,8]{2,1,3,0:T(8,128)} %get-tuple-element.294) | copy-start | bytes 25165828 | tf_op jit(solution)/shard_map/cond/branch_1_fun/while
  139.4 7.9 %copy-start.2 = (s32[4096,512]{1,0:T(8,128)S(1)}, s32[4096,512]{1,0:T(8,128)}, u32[]{:S(2)}) copy-start(s32[4096,512]{1,0:T(8,128)} %all-gather.5.cloned.1.call-done) | copy-start | bytes 25165828
Sparse Core Ops, SparseCore 0:
  9.5 55.1 all-gather.2
  66.9 72.4 all-gather.4
